TPU v7x, 256 devices: a whole 4x4x8 slice. The times are simulated.
256 devices in a mesh: rows: 64 (over x, z, core), cols: 4 (over y).
Axes of the slice: x: 4, y: 4, z: 8, core: 2. Of those that a mesh axis runs over, the one named last changes fastest.
Arguments:
- matrix: bfloat16 [131072, 1024], P('rows', 'cols'), as said below
- row_signs: int32 [131072], P('rows'), may hold values from 0 to 1
- sampled_rows: int32 [64, 2048], P('rows'), may hold values from 0 to 2047
- right_sides: float32 [8, 131072], P(None, 'rows'), may hold values from -6 to 6
Outputs:
- solution: float32 [8, 1024], P(None, 'cols')
- residual: float32 [8, 131072], P(None, 'rows')
Inputs may be any that keep to these rules, and one draw needn't show every extreme that they name: `matrix`: entries are at most 70 / sqrt(131072) in magnitude.
All inputs are finite; a program needn't handle non-finite values.
Results may differ from a plain program's by a relative error of at most 0.0013.
Values sent between devices are 32-bit elements; how exact they have to be, the bound alone decides.
No kernel may reach another device: no remote copies, remote signals or barrier semaphores. Data moves between devices by JAX's collectives and lax.ppermute only.
A program may use at most 64 MiB of HBM per device.

v0:
```python
import math
import jax
import jax.numpy as jnp
from jax import lax
from jax.sharding import PartitionSpec as P

SKETCH = 2048
ROUNDS = 2
highest = lax.Precision.HIGHEST


def split_up(shard, dim, size):
    before, after = (shard.shape[:dim], shard.shape[dim + 1 :])
    return jnp.moveaxis(shard.reshape(*before, size, -1, *after), dim, 0)


def sum_at_owner(shard, axis, dim):
    parts = split_up(shard, dim, lax.axis_size(axis))
    arrived = lax.all_to_all(parts, axis, split_axis=0, concat_axis=0, tiled=True)
    return arrived.sum(axis=0)


def sent_to_all(shard, axis):
    size = lax.axis_size(axis)
    return lax.all_to_all(
        jnp.broadcast_to(shard[None], (size, *shard.shape)), axis, 0, 0, tiled=True
    )


def laid_out(parts, dim):
    lengths = list(parts.shape[1:])
    lengths[dim] *= parts.shape[0]
    return jnp.moveaxis(parts, 0, dim).reshape(lengths)


def gathered_copies(shard, axis, dim):
    parts = sent_to_all(shard, axis)
    return laid_out(parts, dim)


def over_copies(shard, axis):
    everything = sent_to_all(shard, axis)
    return jnp.sum(everything, axis=0)


def in_one(arrays, axis):
    vector, at, finished = (jnp.concatenate([a.reshape(-1) for a in arrays]), 0, [])
    running = over_copies(vector, axis)
    for a in arrays:
        finished.append(running[at : at + a.size].reshape(a.shape))
        at += a.size
    return tuple(finished)


def sylvester(matrix_order):
    positions = jnp.arange(matrix_order, dtype=jnp.int32)
    common = jnp.bitwise_and(positions[:, None], positions[None, :])
    parity = jnp.zeros((matrix_order, matrix_order), jnp.int32)
    for bit_place in range(max(matrix_order.bit_length() - 1, 0)):
        parity = parity + jnp.bitwise_and(jnp.right_shift(common, bit_place), 1)
    return jnp.where(jnp.bitwise_and(parity, 1) == 0, 1.0, -1.0).astype(jnp.float32)


def transform(signed):
    row_count, col_count = signed.shape
    bit_count = row_count.bit_length() - 1
    outer_order = 2 ** (bit_count - bit_count // 2)
    inner_order = row_count // outer_order
    section_one = jnp.dot(
        sylvester(outer_order).astype(jnp.bfloat16),
        signed.reshape(outer_order, inner_order * col_count),
        preferred_element_type=jnp.float32,
    )
    second = jnp.einsum(
        "cd,adn->acn",
        sylvester(inner_order),
        section_one.reshape(outer_order, inner_order, col_count),
        precision=highest,
    )
    return second.reshape(row_count, col_count)


def solve_right(factor, vectors):
    return lax.linalg.triangular_solve(
        factor, vectors, left_side=False, lower=True, transpose_a=True
    )


def solve_left(factor, vectors):
    return lax.linalg.triangular_solve(
        factor, vectors, left_side=False, lower=True, transpose_a=False
    )


def local(matrix, row_signs, sampled_rows, right_sides):
    row_count, col_count = matrix.shape
    systems = right_sides.shape[0]
    flipped = (1 - 2 * row_signs).astype(jnp.bfloat16)
    signed = matrix * flipped[:, None]
    mixed_rows = transform(signed)
    picked = jnp.take(mixed_rows, sampled_rows[0], axis=0) * (1.0 / math.sqrt(SKETCH))
    sketch_piece = sum_at_owner(picked, "rows", 0)
    gram_block = lax.dot_general(
        gathered_copies(sketch_piece, "cols", 1),
        sketch_piece,
        (((0,), (0,)), ((), ())),
        precision=highest,
    )
    gram_band = sum_at_owner(gram_block, "rows", 0)
    gram_strip = gathered_copies(gram_band, "cols", 1)
    gram_matrix = lax.all_gather(gram_strip, "rows", axis=0, tiled=True)
    factor = jnp.linalg.cholesky(gram_matrix)
    col_start = lax.axis_index("cols") * col_count

    def forward(vectors):
        own_part = lax.dynamic_slice_in_dim(vectors, col_start, col_count, 1)
        local_part = lax.dot_general(
            own_part, matrix.astype(jnp.float32), (((1,), (1,)), ((), ())), precision=highest
        )
        return over_copies(local_part, "cols")

    def back_section(forward_rest):
        local_squares = jnp.sum(forward_rest * forward_rest, axis=1)
        local_part = jnp.dot(forward_rest, matrix.astype(jnp.float32), precision=highest)
        summed, total_squares = in_one((local_part, local_squares), "rows")
        beta_norm = jnp.sqrt(total_squares)
        summed = summed / beta_norm[:, None]
        left_unit = forward_rest / beta_norm[:, None]
        whole_vector = gathered_copies(summed, "cols", 1)
        return (beta_norm, left_unit, solve_right(factor, whole_vector))

    beta_norm, left_unit, back_rest = back_section(right_sides)
    alpha_norm = jnp.sqrt(jnp.sum(back_rest * back_rest, axis=1))
    right_unit = back_rest / alpha_norm[:, None]
    search = right_unit
    coeffs = jnp.zeros((systems, back_rest.shape[1]), jnp.float32)
    phibar = beta_norm
    rhobar = alpha_norm
    for iteration in range(ROUNDS):
        forward_rest = forward(solve_left(factor, right_unit)) - alpha_norm[:, None] * left_unit
        beta_norm, left_unit, back_rest = back_section(forward_rest)
        back_rest = back_rest - beta_norm[:, None] * right_unit
        alpha_norm = jnp.sqrt(jnp.sum(back_rest * back_rest, axis=1))
        right_unit = back_rest / alpha_norm[:, None]
        rho_total = jnp.sqrt(rhobar * rhobar + beta_norm * beta_norm)
        cosine = rhobar / rho_total
        sine_part = beta_norm / rho_total
        theta_term = sine_part * alpha_norm
        rhobar = -cosine * alpha_norm
        phi_term = cosine * phibar
        phibar = sine_part * phibar
        coeffs = coeffs + (phi_term / rho_total)[:, None] * search
        search = right_unit - (theta_term / rho_total)[:, None] * search
    full_solution = solve_left(factor, coeffs)
    residual = right_sides - forward(full_solution)
    solution = lax.dynamic_slice_in_dim(full_solution, col_start, col_count, 1)
    return (solution, residual)


def solution(mesh):
    in_specs = (P("rows", "cols"), P("rows"), P("rows", None), P(None, "rows"))
    out_specs = (P(None, "cols"), P(None, "rows"))
    return jax.shard_map(local, mesh=mesh, in_specs=in_specs, out_specs=out_specs, check_vma=False)
```

profile of v0, /device:TPU:1, one launch (start us, length us, event | category | flops | bytes accessed | tf_op | source)
XLA Modules:
  0.0 691.9 jit_solution(14446551683061149268)
XLA Ops:
  25.3 64.0 %all_to_all.63 = f32[64,32,256]{2,1,0:T(8,128)S(1)} all-to-all(f32[64,32,256]{2,1,0:T(8,128)S(1)} %select_multiply_fusion), channel_id=1, replica_groups=mesh['rows'=64,'cols'=4] {'rows'}, dimensions={0} | all-to-all | bytes 4194304 | tf_op jit(solution)/shard_map/all_to_all | solution.py:19
  99.6 35.6 %all_to_all.65 = f32[64,16,256]{2,1,0:T(8,128)S(1)} all-to-all(f32[64,16,256]{2,1,0:T(8,128)S(1)} %fusion.103), channel_id=1, replica_groups=mesh['rows'=64,'cols'=4] {'rows'}, dimensions={0} | all-to-all | bytes 2097152 | tf_op jit(solution)/shard_map/all_to_all | solution.py:19
  152.0 19.4 %all-to-all-done.4 = f32[64,1,2056]{2,1,0:T(1,128)S(1)} async-done(((f32[64,1,2056]{2,1,0:T(1,128)}), f32[64,1,2056]{2,1,0:T(1,128)S(1)}, u32[]{:S(2)}, u32[]{:S(2)}) %all-to-all-start.4) | async-done | bytes 526368 | tf_op jit(solution)/shard_map/all_to_all | solution.py:25
  175.7 43.4 %all-gather.2.cloned.1.call-done = f32[1024,1024]{1,0:T(8,128)} async-done(((f32[16,1024]{1,0:T(8,128)}), f32[1024,1024]{1,0:T(8,128)}) %all-gather.2.cloned.1.call-update) | async-done | bytes 4194320 | tf_op jit(solution)/shard_map/all_gather | solution.py:111
  231.0 11.7 %cholesky.223 = f32[128,128]{1,0:T(8,128)S(1)} custom-call(f32[128,128]{1,0:T(8,128)S(1)} %cholesky.580), custom_call_target="Cholesky" | custom-call | tf_op jit(solution)/shard_map/jit(cholesky)/cholesky | solution.py:112
  245.2 9.8 %custom-call.65 = f32[1,128,128]{1,2,0:T(8,128)S(1)} custom-call(f32[1,128,128]{2,1,0:T(8,128)S(1)} %get-tuple-element.83), custom_call_target="InvertDiagBlocksLowerTriangular" | custom-call | tf_op jit(solution)/shard_map/jit(cholesky)/cholesky | solution.py:112
  259.0 11.9 %cholesky.244 = f32[128,128]{1,0:T(8,128)S(1)} custom-call(f32[128,128]{1,0:T(8,128)S(1)} %cholesky.584), custom_call_target="Cholesky" | custom-call | tf_op jit(solution)/shard_map/jit(cholesky)/cholesky | solution.py:112
  271.5 9.8 %custom-call.66 = f32[1,128,128]{1,2,0:T(8,128)S(1)} custom-call(f32[1,128,128]{2,1,0:T(8,128)S(1)} %get-tuple-element.80), custom_call_target="InvertDiagBlocksLowerTriangular" | custom-call | tf_op jit(solution)/shard_map/jit(cholesky)/cholesky | solution.py:112
  284.7 11.7 %cholesky.468 = f32[128,128]{1,0:T(8,128)S(1)} custom-call(f32[128,128]{1,0:T(8,128)S(1)} %cholesky.589), custom_call_target="Cholesky" | custom-call | tf_op jit(solution)/shard_map/jit(cholesky)/cholesky | solution.py:112
  297.7 9.8 %custom-call.67 = f32[1,128,128]{1,2,0:T(8,128)S(1)} custom-call(f32[1,128,128]{2,1,0:T(8,128)S(1)} %get-tuple-element.77), custom_call_target="InvertDiagBlocksLowerTriangular" | custom-call | tf_op jit(solution)/shard_map/jit(cholesky)/cholesky | solution.py:112
  311.0 12.1 %cholesky.487 = f32[128,128]{1,0:T(8,128)S(1)} custom-call(f32[128,128]{1,0:T(8,128)S(1)} %cholesky.594), custom_call_target="Cholesky" | custom-call | tf_op jit(solution)/shard_map/jit(cholesky)/cholesky | solution.py:112
  324.4 9.8 %custom-call.68 = f32[1,128,128]{1,2,0:T(8,128)S(1)} custom-call(f32[1,128,128]{2,1,0:T(8,128)S(1)} %get-tuple-element.74), custom_call_target="InvertDiagBlocksLowerTriangular" | custom-call | tf_op jit(solution)/shard_map/jit(cholesky)/cholesky | solution.py:112
  337.7 11.7 %cholesky.506 = f32[128,128]{1,0:T(8,128)S(1)} custom-call(f32[128,128]{1,0:T(8,128)S(1)} %cholesky.599), custom_call_target="Cholesky" | custom-call | tf_op jit(solution)/shard_map/jit(cholesky)/cholesky | solution.py:112
  350.6 9.9 %custom-call.69 = f32[1,128,128]{1,2,0:T(8,128)S(1)} custom-call(f32[1,128,128]{2,1,0:T(8,128)S(1)} %get-tuple-element.71), custom_call_target="InvertDiagBlocksLowerTriangular" | custom-call | tf_op jit(solution)/shard_map/jit(cholesky)/cholesky | solution.py:112
  363.9 11.7 %cholesky.526 = f32[128,128]{1,0:T(8,128)S(1)} custom-call(f32[128,128]{1,0:T(8,128)S(1)} %cholesky.604), custom_call_target="Cholesky" | custom-call | tf_op jit(solution)/shard_map/jit(cholesky)/cholesky | solution.py:112
  376.9 9.8 %custom-call.70 = f32[1,128,128]{1,2,0:T(8,128)S(1)} custom-call(f32[1,128,128]{2,1,0:T(8,128)S(1)} %get-tuple-element.68), custom_call_target="InvertDiagBlocksLowerTriangular" | custom-call | tf_op jit(solution)/shard_map/jit(cholesky)/cholesky | solution.py:112
  389.7 11.9 %cholesky.546 = f32[128,128]{1,0:T(8,128)S(1)} custom-call(f32[128,128]{1,0:T(8,128)S(1)} %cholesky.609), custom_call_target="Cholesky" | custom-call | tf_op jit(solution)/shard_map/jit(cholesky)/cholesky | solution.py:112
  403.0 9.8 %custom-call.71 = f32[1,128,128]{1,2,0:T(8,128)S(1)} custom-call(f32[1,128,128]{2,1,0:T(8,128)S(1)} %get-tuple-element.65), custom_call_target="InvertDiagBlocksLowerTriangular" | custom-call | tf_op jit(solution)/shard_map/jit(cholesky)/cholesky | solution.py:112
  415.4 11.7 %cholesky.564 = f32[128,128]{1,0:T(8,128)S(1)} custom-call(f32[128,128]{1,0:T(8,128)S(1)} %convolution_subtract_fusion.6), custom_call_target="Cholesky" | custom-call | tf_op jit(solution)/shard_map/jit(cholesky)/cholesky | solution.py:112
  438.8 23.0 %while.10 = (s32[]{:T(128)}, f32[1024,1024]{1,0:T(8,128)}, s32[8,2]{0,1:T(2,128)S(1)}, f32[8,128,128]{2,1,0:T(8,128)S(1)}, s32[]{:T(128)}) while((s32[]{:T(128)}, f32[1024,1024]{1,0:T(8,128)}, s32[8,2]{0,1:T(2,128)S(1)}, f32[8,128,128]{2,1,0:T(8,128)S(1)}, s32[]{:T(128)}) %tuple.114), condition=%wide.while_cond, body=%wide.while_body.sunk | while | flops 2 | bytes 131181 | solution.py:84
  461.8 79.0 %custom-call.75 = f32[8,128,128]{1,2,0:T(8,128)S(1)} custom-call(f32[8,128,128]{2,1,0:T(8,128)S(1)} %get-tuple-element.38), custom_call_target="InvertDiagBlocksLowerTriangular" | custom-call | tf_op jit(solution)/shard_map/triangular_solve/custom-call.7 | solution.py:84
  562.8 10.0 %all_to_all.67 = f32[4,8,2048]{2,1,0:T(8,128)S(1)} all-to-all(f32[4,8,2048]{2,1,0:T(8,128)S(1)} %broadcast_in_dim.58), channel_id=1, replica_groups=mesh['rows'=64,'cols'=4] {'cols'}, dimensions={0} | all-to-all | bytes 524288 | tf_op jit(solution)/shard_map/all_to_all | solution.py:25
  573.9 25.1 %all_to_all.68 = f32[64,1,2056]{2,1,0:T(1,128)S(1)} all-to-all(f32[64,1,2056]{2,1,0:T(1,128)S(1)} %broadcast_in_dim.59), channel_id=1, replica_groups=mesh['rows'=64,'cols'=4] {'rows'}, dimensions={0} | all-to-all | bytes 1052672 | tf_op jit(solution)/shard_map/all_to_all | solution.py:25
  637.3 26.4 %all_to_all.71 = f32[64,1,2056]{2,1,0:T(1,128)S(1)} all-to-all(f32[64,1,2056]{2,1,0:T(1,128)S(1)} %broadcast_in_dim.62), channel_id=1, replica_groups=mesh['rows'=64,'cols'=4] {'rows'}, dimensions={0} | all-to-all | bytes 1052672 | tf_op jit(solution)/shard_map/all_to_all | solution.py:25
  (297 shorter events, 205.4 us)
Async XLA Ops:
  7.2 211.9 %all-gather.2.cloned.1.call-start = ((), (), s32[]{:S(2)}) async-start(), calls=%async_computation.12 | async-start | bytes 4259840 | tf_op jit(solution)/shard_map/all_gather | solution.py:111
  10.0 3.7 copy-start.4
  89.3 53.5 %copy-start = (bf16[2048,256]{1,0:T(8,128)(2,1)S(1)}, bf16[2048,256]{1,0:T(8,128)(2,1)}, u32[]{:S(2)}) copy-start(bf16[2048,256]{1,0:T(8,128)(2,1)} %param.8) | copy-start | bytes 3145732
  89.3 53.5 %copy-start.2 = (f32[8,2048]{1,0:T(8,128)S(1)}, f32[8,2048]{1,0:T(8,128)}, u32[]{:S(2)}) copy-start(f32[8,2048]{1,0:T(8,128)} %param.11) | copy-start | bytes 196612
  144.6 26.8 %all-to-all-start.4 = ((f32[64,1,2056]{2,1,0:T(1,128)}), f32[64,1,2056]{2,1,0:T(1,128)S(1)}, u32[]{:S(2)}, u32[]{:S(2)}) async-start(f32[64,1,2056]{2,1,0:T(1,128)} %broadcast_in_dim.56), calls=%async_computation.4 | async-start | bytes 1114112 | tf_op jit(solution)/shard_map/all_to_all | solution.py:25
  172.4 368.4 %all-to-all-start.5 = ((f32[4,8,256]{2,1,0:T(8,128)}), f32[4,8,256]{2,1,0:T(8,128)S(1)}, u32[]{:S(2)}, u32[]{:S(2)}) async-start(f32[4,8,256]{2,1,0:T(8,128)} %broadcast_in_dim.57), calls=%async_computation.5 | async-start | bytes 65536 | tf_op jit(solution)/shard_map/all_to_all | solution.py:25
  229.0 1.9 copy-start.1
  674.5 10.4 %copy-start.3 = (f32[8,256]{1,0:T(8,128)}, f32[8,256]{1,0:T(8,128)S(1)}, u32[]{:S(2)}) copy-start(f32[8,256]{1,0:T(8,128)S(1)} %constant_dynamic-slice_fusion.1) | copy-start | bytes 24580
Sparse Core Ops, SparseCore 0:
  142.9 76.1 all-gather.1
where the time goes:
time: 702 us; the launch traced here: 692 us
  other arithmetic  269 us (38%)
  blocking collectives  200 us (28%)
  matrix products  82.7 us (12%)
  waiting for transfers between devices  62.8 us (9%)
  local copies, waits for them, and re-layouts  46.3 us (7%)
  between operations  20.3 us (3%)
  starting transfers between devices  10.6 us (2%)
    another operation x30, other arithmetic, local(): factor = jnp.linalg.cholesky(gram_matrix)  172 us
    all_to_all x8, blocking collectives, sent_to_all(): lax.all_to_all(jnp.broadcast_to(shard[None], (size, *shard.shape)), axis,...  101 us
    all_to_all x2, blocking collectives, sum_at_owner(): lax.all_to_all(parts, axis, split_axis=0, concat_axis=0, tiled=True)  99.5 us
    another operation x4, other arithmetic, solve_right(): lax.linalg.triangular_solve(factor, vectors, left_side=False, lower=True,...  83.8 us
    all_gather x1, waiting for transfers between devices, local(): gram_matrix = lax.all_gather(gram_strip, 'rows', axis=0, tiled=True)  43.4 us
    another operation x45, matrix products, solve_left(): lax.linalg.triangular_solve(factor, vectors, left_side=False, lower=True,...  29.9 us
    another operation x14, matrix products, local(): factor = jnp.linalg.cholesky(gram_matrix)  23.1 us
    another operation x25, local copies, waits for them, and re-layouts, solve_right(): lax.linalg.triangular_solve(factor, vectors, left_side=False, lower=True,...  22.8 us
  transfers between devices with their start and end apart: 3, of which 2 were waited for; matrix products, arithmetic and copies ran while one was open for 46% of the time, Pallas kernels for 0%

commit v1 on v0

--- a/solution.py
+++ b/solution.py
@@ -7,6 +7,12 @@
 SKETCH = 2048
 ROUNDS = 2
 highest = lax.Precision.HIGHEST
+
+
+def gather_by_exchange(x, axis, dim):
+    devices = lax.axis_size(axis)
+    repeats = [devices if d == dim else 1 for d in range(x.ndim)]
+    return lax.all_to_all(jnp.tile(x, repeats), axis, split_axis=dim, concat_axis=dim, tiled=True)
 
 
 def split_up(shard, dim, size):
@@ -108,7 +114,7 @@
     )
     gram_band = sum_at_owner(gram_block, "rows", 0)
     gram_strip = gathered_copies(gram_band, "cols", 1)
-    gram_matrix = lax.all_gather(gram_strip, "rows", axis=0, tiled=True)
+    gram_matrix = gather_by_exchange(gram_strip, "rows", 0)
     factor = jnp.linalg.cholesky(gram_matrix)
     col_start = lax.axis_index("cols") * col_count
 

time: 702 us -> 751 us (1.070)
  waiting for transfers between devices: 62.8 us -> 146 us
  blocking collectives: 200 us -> 158 us
  starting transfers between devices: 10.6 us -> 27.6 us
  between operations: 20.3 us -> 7.06 us
    all_to_all x0 -> x2, waiting for transfers between devices: none -> 123 us  [the longest x1 95.4 us: gather_by_exchange(): lax.all_to_all(jnp.tile(x, repeats), axis, split_axis=dim, concat_axis=di...]
    all_gather x1 -> x0, waiting for transfers between devices: 43.4 us -> none  [local(): gram_matrix = lax.all_gather(gram_strip, 'rows', axis=0, tiled=True)]
    all_to_all x2 -> x1, blocking collectives: 99.5 us -> 64 us  [sum_at_owner(): lax.all_to_all(parts, axis, split_axis=0, concat_axis=0, tiled=True)]
    all_to_all x0 -> x2, starting transfers between devices: none -> 13.7 us  [the longest x1 7.26 us: sum_at_owner(): lax.all_to_all(parts, axis, split_axis=0, concat_axis=0, tiled=True)]
    all_to_all x8 -> x7, blocking collectives: 101 us -> 94 us  [sent_to_all(): lax.all_to_all(jnp.broadcast_to(shard[None], (size, *shard.shape)), axis,...]
    all_to_all x2 -> x3, waiting for transfers between devices: 19.4 us -> 22.5 us  [sent_to_all(): lax.all_to_all(jnp.broadcast_to(shard[None], (size, *shard.shape)), axis,...]
  transfers between devices with their start and end apart: 3 -> 5, of which waited for: 2 -> 4; matrix products, arithmetic and copies ran while one was open for 46% -> 43% of each run, Pallas kernels for 0% -> 0%
where the time goes in v1:
time: 751 us; the launch traced here: 739 us
  other arithmetic  268 us (36%)
  blocking collectives  158 us (21%)
  waiting for transfers between devices  146 us (19%)
  matrix products  83.7 us (11%)
  local copies, waits for them, and re-layouts  48.9 us (7%)
  starting transfers between devices  27.6 us (4%)
    another operation x30, other arithmetic, local(): factor = jnp.linalg.cholesky(gram_matrix)  172 us
    all_to_all x1, waiting for transfers between devices, gather_by_exchange(): lax.all_to_all(jnp.tile(x, repeats), axis, split_axis=dim, concat_axis=di...  95.4 us
    all_to_all x7, blocking collectives, sent_to_all(): lax.all_to_all(jnp.broadcast_to(shard[None], (size, *shard.shape)), axis,...  94 us
    another operation x4, other arithmetic, solve_right(): lax.linalg.triangular_solve(factor, vectors, left_side=False, lower=True,...  83.6 us
    all_to_all x1, blocking collectives, sum_at_owner(): lax.all_to_all(parts, axis, split_axis=0, concat_axis=0, tiled=True)  64 us
    another operation x45, matrix products, solve_left(): lax.linalg.triangular_solve(factor, vectors, left_side=False, lower=True,...  29.9 us
    all_to_all x1, waiting for transfers between devices, sum_at_owner(): lax.all_to_all(parts, axis, split_axis=0, concat_axis=0, tiled=True)  27.8 us
    another operation x14, matrix products, local(): factor = jnp.linalg.cholesky(gram_matrix)  23.1 us
  transfers between devices with their start and end apart: 5, of which 4 were waited for; matrix products, arithmetic and copies ran while one was open for 43% of the time, Pallas kernels for 0%

profile of v1, /device:TPU:1, one launch (start us, length us, event | category | flops | bytes accessed | tf_op | source)
XLA Modules:
  0.0 739.2 jit_solution(12663677279429568933)
XLA Ops:
  18.8 64.0 %all_to_all.72 = f32[64,32,256]{2,1,0:T(8,128)S(1)} all-to-all(f32[64,32,256]{2,1,0:T(8,128)S(1)} %select_multiply_fusion), channel_id=1, replica_groups=mesh['rows'=64,'cols'=4] {'rows'}, dimensions={0} | all-to-all | bytes 4194304 | tf_op jit(solution)/shard_map/all_to_all | solution.py:25
  102.0 27.8 %all-to-all-done.2 = f32[64,16,256]{2,1,0:T(8,128)S(1)} async-done(((f32[64,16,256]{2,1,0:T(8,128)}), f32[64,16,256]{2,1,0:T(8,128)S(1)}, u32[]{:S(2)}, u32[]{:S(2)}) %all-to-all-start.2) | async-done | bytes 1048608 | tf_op jit(solution)/shard_map/all_to_all | solution.py:25
  146.7 18.0 %all-to-all-done.5 = f32[64,1,2056]{2,1,0:T(1,128)S(1)} async-done(((f32[64,1,2056]{2,1,0:T(1,128)}), f32[64,1,2056]{2,1,0:T(1,128)S(1)}, u32[]{:S(2)}, u32[]{:S(2)}) %all-to-all-start.5) | async-done | bytes 526368 | tf_op jit(solution)/shard_map/all_to_all | solution.py:31
  174.2 95.4 %all-to-all-done.4 = f32[64,16,1024]{2,1,0:T(8,128)} async-done(((f32[64,16,1024]{2,1,0:T(8,128)}), f32[64,16,1024]{2,1,0:T(8,128)}, u32[]{:S(2)}, u32[]{:S(2)}) %all-to-all-start.4) | async-done | bytes 4194336 | tf_op jit(solution)/shard_map/all_to_all | solution.py:15
  285.5 11.7 %cholesky.223 = f32[128,128]{1,0:T(8,128)S(1)} custom-call(f32[128,128]{1,0:T(8,128)S(1)} %cholesky.580), custom_call_target="Cholesky" | custom-call | tf_op jit(solution)/shard_map/jit(cholesky)/cholesky | solution.py:118
  299.7 9.8 %custom-call.65 = f32[1,128,128]{1,2,0:T(8,128)S(1)} custom-call(f32[1,128,128]{2,1,0:T(8,128)S(1)} %get-tuple-element.83), custom_call_target="InvertDiagBlocksLowerTriangular" | custom-call | tf_op jit(solution)/shard_map/jit(cholesky)/cholesky | solution.py:118
  313.5 11.9 %cholesky.244 = f32[128,128]{1,0:T(8,128)S(1)} custom-call(f32[128,128]{1,0:T(8,128)S(1)} %cholesky.584), custom_call_target="Cholesky" | custom-call | tf_op jit(solution)/shard_map/jit(cholesky)/cholesky | solution.py:118
  326.0 9.8 %custom-call.66 = f32[1,128,128]{1,2,0:T(8,128)S(1)} custom-call(f32[1,128,128]{2,1,0:T(8,128)S(1)} %get-tuple-element.80), custom_call_target="InvertDiagBlocksLowerTriangular" | custom-call | tf_op jit(solution)/shard_map/jit(cholesky)/cholesky | solution.py:118
  339.1 11.7 %cholesky.468 = f32[128,128]{1,0:T(8,128)S(1)} custom-call(f32[128,128]{1,0:T(8,128)S(1)} %cholesky.589), custom_call_target="Cholesky" | custom-call | tf_op jit(solution)/shard_map/jit(cholesky)/cholesky | solution.py:118
  352.1 9.8 %custom-call.67 = f32[1,128,128]{1,2,0:T(8,128)S(1)} custom-call(f32[1,128,128]{2,1,0:T(8,128)S(1)} %get-tuple-element.77), custom_call_target="InvertDiagBlocksLowerTriangular" | custom-call | tf_op jit(solution)/shard_map/jit(cholesky)/cholesky | solution.py:118
  365.4 11.9 %cholesky.487 = f32[128,128]{1,0:T(8,128)S(1)} custom-call(f32[128,128]{1,0:T(8,128)S(1)} %cholesky.594), custom_call_target="Cholesky" | custom-call | tf_op jit(solution)/shard_map/jit(cholesky)/cholesky | solution.py:118
  378.6 9.8 %custom-call.68 = f32[1,128,128]{1,2,0:T(8,128)S(1)} custom-call(f32[1,128,128]{2,1,0:T(8,128)S(1)} %get-tuple-element.74), custom_call_target="InvertDiagBlocksLowerTriangular" | custom-call | tf_op jit(solution)/shard_map/jit(cholesky)/cholesky | solution.py:118
  391.9 11.7 %cholesky.506 = f32[128,128]{1,0:T(8,128)S(1)} custom-call(f32[128,128]{1,0:T(8,128)S(1)} %cholesky.599), custom_call_target="Cholesky" | custom-call | tf_op jit(solution)/shard_map/jit(cholesky)/cholesky | solution.py:118
  404.9 10.2 %custom-call.69 = f32[1,128,128]{1,2,0:T(8,128)S(1)} custom-call(f32[1,128,128]{2,1,0:T(8,128)S(1)} %get-tuple-element.71), custom_call_target="InvertDiagBlocksLowerTriangular" | custom-call | tf_op jit(solution)/shard_map/jit(cholesky)/cholesky | solution.py:118
  418.4 11.7 %cholesky.526 = f32[128,128]{1,0:T(8,128)S(1)} custom-call(f32[128,128]{1,0:T(8,128)S(1)} %cholesky.604), custom_call_target="Cholesky" | custom-call | tf_op jit(solution)/shard_map/jit(cholesky)/cholesky | solution.py:118
  431.4 9.8 %custom-call.70 = f32[1,128,128]{1,2,0:T(8,128)S(1)} custom-call(f32[1,128,128]{2,1,0:T(8,128)S(1)} %get-tuple-element.68), custom_call_target="InvertDiagBlocksLowerTriangular" | custom-call | tf_op jit(solution)/shard_map/jit(cholesky)/cholesky | solution.py:118
  444.2 11.9 %cholesky.546 = f32[128,128]{1,0:T(8,128)S(1)} custom-call(f32[128,128]{1,0:T(8,128)S(1)} %cholesky.609), custom_call_target="Cholesky" | custom-call | tf_op jit(solution)/shard_map/jit(cholesky)/cholesky | solution.py:118
  457.3 9.8 %custom-call.71 = f32[1,128,128]{1,2,0:T(8,128)S(1)} custom-call(f32[1,128,128]{2,1,0:T(8,128)S(1)} %get-tuple-element.65), custom_call_target="InvertDiagBlocksLowerTriangular" | custom-call | tf_op jit(solution)/shard_map/jit(cholesky)/cholesky | solution.py:118
  469.7 11.7 %cholesky.564 = f32[128,128]{1,0:T(8,128)S(1)} custom-call(f32[128,128]{1,0:T(8,128)S(1)} %convolution_subtract_fusion.6), custom_call_target="Cholesky" | custom-call | tf_op jit(solution)/shard_map/jit(cholesky)/cholesky | solution.py:118
  493.1 22.8 %while.10 = (s32[]{:T(128)}, f32[1024,1024]{1,0:T(8,128)}, s32[8,2]{0,1:T(2,128)S(1)}, f32[8,128,128]{2,1,0:T(8,128)S(1)}, s32[]{:T(128)}) while((s32[]{:T(128)}, f32[1024,1024]{1,0:T(8,128)}, s32[8,2]{0,1:T(2,128)S(1)}, f32[8,128,128]{2,1,0:T(8,128)S(1)}, s32[]{:T(128)}) %tuple.114), condition=%wide.while_cond, body=%wide.while_body.sunk | while | flops 2 | bytes 131181 | solution.py:90
  515.9 78.8 %custom-call.75 = f32[8,128,128]{1,2,0:T(8,128)S(1)} custom-call(f32[8,128,128]{2,1,0:T(8,128)S(1)} %get-tuple-element.38), custom_call_target="InvertDiagBlocksLowerTriangular" | custom-call | tf_op jit(solution)/shard_map/triangular_solve/custom-call.7 | solution.py:90
  616.7 9.7 %all_to_all.74 = f32[4,8,2048]{2,1,0:T(8,128)S(1)} all-to-all(f32[4,8,2048]{2,1,0:T(8,128)S(1)} %broadcast_in_dim.58), channel_id=1, replica_groups=mesh['rows'=64,'cols'=4] {'cols'}, dimensions={0} | all-to-all | bytes 524288 | tf_op jit(solution)/shard_map/all_to_all | solution.py:31
  627.4 25.4 %all_to_all.75 = f32[64,1,2056]{2,1,0:T(1,128)S(1)} all-to-all(f32[64,1,2056]{2,1,0:T(1,128)S(1)} %broadcast_in_dim.59), channel_id=1, replica_groups=mesh['rows'=64,'cols'=4] {'rows'}, dimensions={0} | all-to-all | bytes 1052672 | tf_op jit(solution)/shard_map/all_to_all | solution.py:31
  691.2 26.4 %all_to_all.78 = f32[64,1,2056]{2,1,0:T(1,128)S(1)} all-to-all(f32[64,1,2056]{2,1,0:T(1,128)S(1)} %broadcast_in_dim.62), channel_id=1, replica_groups=mesh['rows'=64,'cols'=4] {'rows'}, dimensions={0} | all-to-all | bytes 1052672 | tf_op jit(solution)/shard_map/all_to_all | solution.py:31
  (299 shorter events, 223.4 us)
Async XLA Ops:
  3.4 3.7 copy-start.4
  82.7 18.6 %copy-start = (bf16[2048,256]{1,0:T(8,128)(2,1)S(1)}, bf16[2048,256]{1,0:T(8,128)(2,1)}, u32[]{:S(2)}) copy-start(bf16[2048,256]{1,0:T(8,128)(2,1)} %param.8) | copy-start | bytes 3145732
  82.7 18.6 %copy-start.2 = (f32[8,2048]{1,0:T(8,128)S(1)}, f32[8,2048]{1,0:T(8,128)}, u32[]{:S(2)}) copy-start(f32[8,2048]{1,0:T(8,128)} %param.11) | copy-start | bytes 196612
  94.0 35.8 %all-to-all-start.2 = ((f32[64,16,256]{2,1,0:T(8,128)}), f32[64,16,256]{2,1,0:T(8,128)S(1)}, u32[]{:S(2)}, u32[]{:S(2)}) async-start(f32[64,16,256]{2,1,0:T(8,128)} %fusion.103), calls=%async_computation.2 | async-start | bytes 2097152 | tf_op jit(solution)/shard_map/all_to_all | solution.py:25
  130.5 7.7 %all-to-all-start.3 = ((f32[4,16,256]{2,1,0:T(8,128)}), f32[4,16,256]{2,1,0:T(8,128)S(1)}, u32[]{:S(2)}, u32[]{:S(2)}) async-start(f32[4,16,256]{2,1,0:T(8,128)} %broadcast_in_dim.55), calls=%async_computation.3 | async-start | bytes 131072 | tf_op jit(solution)/shard_map/all_to_all | solution.py:31
  139.4 25.4 %all-to-all-start.5 = ((f32[64,1,2056]{2,1,0:T(1,128)}), f32[64,1,2056]{2,1,0:T(1,128)S(1)}, u32[]{:S(2)}, u32[]{:S(2)}) async-start(f32[64,1,2056]{2,1,0:T(1,128)} %broadcast_in_dim.56), calls=%async_computation.5 | async-start | bytes 1114112 | tf_op jit(solution)/shard_map/all_to_all | solution.py:31
  167.2 102.3 %all-to-all-start.4 = ((f32[64,16,1024]{2,1,0:T(8,128)}), f32[64,16,1024]{2,1,0:T(8,128)}, u32[]{:S(2)}, u32[]{:S(2)}) async-start(f32[64,16,1024]{2,1,0:T(8,128)} %tile.9), calls=%async_computation.4 | async-start | bytes 8388608 | tf_op jit(solution)/shard_map/all_to_all | solution.py:15
  270.1 324.6 %all-to-all-start.6 = ((f32[4,8,256]{2,1,0:T(8,128)}), f32[4,8,256]{2,1,0:T(8,128)S(1)}, u32[]{:S(2)}, u32[]{:S(2)}) async-start(f32[4,8,256]{2,1,0:T(8,128)} %broadcast_in_dim.57), calls=%async_computation.6 | async-start | bytes 65536 | tf_op jit(solution)/shard_map/all_to_all | solution.py:31
  283.5 1.9 copy-start.1
  728.4 10.4 %copy-start.3 = (f32[8,256]{1,0:T(8,128)}, f32[8,256]{1,0:T(8,128)S(1)}, u32[]{:S(2)}) copy-start(f32[8,256]{1,0:T(8,128)S(1)} %constant_dynamic-slice_fusion.1) | copy-start | bytes 24580
